TPU v7x, 256 devices: a 2x2x32 block of a 4x8x32 slice. The times are simulated.
256 devices in a mesh: rep: 4 (over y, x), bx: 64 (over z, core).
Axes of the slice: x: 2, y: 2, z: 32, core: 2. Of those that a mesh axis runs over, the one named last changes fastest.
The devices are a block of a 4x8x32 slice.
Arguments:
- positions: float32 [1024, 3, 128], P(('rep', 'bx')), parts along dimension 0, may hold values from 0 to 4.5
- species: int32 [1024, 128], P(('rep', 'bx')), parts along dimension 0, may hold values from 0 to 88
- element_embed: bfloat16 [89, 128], replicated, may hold values from -6 to 6
- radial_one: float32 [8, 128], replicated, may hold values from -2 to 2
- mix_one: bfloat16 [128, 128], replicated, may hold values from -0.5 to 0.5
- radial_two: float32 [8, 128], replicated, may hold values from -2 to 2
- mix_two: bfloat16 [128, 128], replicated, may hold values from -0.5 to 0.5
- readout: bfloat16 [128], replicated, may hold values from -0.5 to 0.5
- tile_list: int32 [3072, 2], P(('rep', 'bx')), parts along dimension 0, may hold values from 0 to 7, as said below
- tile_count: int32 [256], P(('rep', 'bx')), parts along dimension 0, may hold values from 4 to 12, as said below
- border: int32 [512, 2], P(('rep', 'bx')), parts along dimension 0, may hold values from 0 to 3, as said below
Outputs:
- atom_energy: float32 [1024, 128], P(('rep', 'bx')), parts along dimension 0
- forces: float32 [1024, 3, 128], P(('rep', 'bx')), parts along dimension 0
- descriptors: bfloat16 [1024, 4, 128, 128], P(('rep', 'bx')), parts along dimension 0
There are 4 independent parts, one for each index of `rep`. A program takes and returns all parts, laid end to end along the dimension named above; an argument that names none is the same for every part. Nothing has to cross between parts.
Inputs may be any that keep to these rules, and one draw needn't show every extreme that they name: `tile_list`: row 12 d + t belongs to slab d: its first entry is a cluster of that slab (0 to 3), its second a position in ext_d (0 to 7). `tile_count`: live tiles of a slab; 12 on at least one slab of every draw. `border`: rows 2 d and 2 d + 1 list distinct clusters of slab d, sent to its left and to its right neighbour.
All inputs are finite; a program needn't handle non-finite values.
Results may differ from a plain program's by a relative error of at most 0.0058.
Values may be sent and summed in bfloat16 or wider, within the bound.
A program may use at most 64 MiB of HBM per device.

v0:
```python
import functools
import math

import jax
import jax.numpy as jnp
from jax import lax
from jax.experimental import pallas as pl
from jax.experimental.pallas import tpu as pltpu
from jax.sharding import PartitionSpec as P

MESH = pl.DeviceIdType.MESH
F32 = jnp.float32
BF16 = jnp.bfloat16

soften = 0.25
cutoff = 3.6
spread = 0.9
first_center = 0.25
center_step = 0.45
message_scale = 0.125
ratio = center_step / spread

NN = (((1,), (0,)), ((), ()))
NT = (((1,), (1,)), ((), ()))
TN = (((0,), (0,)), ((), ()))


def dot(a, b, dims=NN):
    return lax.dot_general(a, b, dims, preferred_element_type=F32)


def split(value):
    high = value.astype(BF16)
    return high, (value - high.astype(F32)).astype(BF16)


def body(
    sizes,
    tiles_ref,
    count_ref,
    border_ref,
    pos_far,
    species_far,
    embed_far,
    radial_one_far,
    mix_one_far,
    radial_two_far,
    mix_two_far,
    readout_far,
    energy_ref,
    forces_ref,
    desc_ref,
    links,
    pos_ref,
    species_ref,
    embed_ref,
    radial_one_ref,
    mix_one_ref,
    radial_two_ref,
    mix_two_ref,
    readout_ref,
    load_sem,
    send_pos,
    recv_pos,
    send_feat,
    recv_feat,
    send_grad,
    recv_grad,
    recv_move,
    pos_ext,
    spread_pos,
    scale_one,
    scale_two,
    feat_t,
    feat,
    lift_one,
    layer_t,
    layer,
    kern,
    radial,
    direction,
    total,
    second,
    adj_two,
    adj_two_t,
    adj_one_t,
    direct,
    moves,
    send_sem,
    recv_sem,
):
    n, clusters, margin, cap, bases, size = sizes
    ext = clusters + 2 * margin
    me = lax.axis_index("bx")
    rep = lax.axis_index("rep")
    right = lax.rem(me + 1, n)
    left = lax.rem(me + n - 1, n)

    def cols(i, width=1):
        return slice(i * size, (i + width) * size)

    def exchange(step, src_left, src_right, dst):
        out = []
        for side, (src, target) in enumerate(((src_left, left), (src_right, right))):
            copy = pltpu.make_async_remote_copy(
                src_ref=src,
                dst_ref=dst[1 - side],
                send_sem=send_sem.at[step, side],
                recv_sem=recv_sem.at[step, 1 - side],
                device_id=(rep, target),
                device_id_type=MESH,
            )
            copy.start()
            out.append(copy)
        return out

    def finish(copies):
        for copy in copies:
            copy.wait()

    far = (
        pos_far, species_far, embed_far, radial_one_far, mix_one_far, radial_two_far, mix_two_far, readout_far
    )
    near = (
        pos_ref, species_ref, embed_ref, radial_one_ref, mix_one_ref, radial_two_ref, mix_two_ref, readout_ref
    )
    loads = [
        pltpu.make_async_copy(src, dst, load_sem.at[i])
        for i, (src, dst) in enumerate(zip(far, near, strict=True))
    ]
    for load in loads:
        load.start()
    barrier = pltpu.get_barrier_semaphore()
    for neighbour in (left, right):
        pl.semaphore_signal(barrier, inc=1, device_id=(rep, neighbour), device_id_type=MESH)

    for load in loads:
        load.wait()
    for side in range(2):
        for s in range(margin):
            which = border_ref[side, s]
            for e in range(3):
                send_pos[side, s, e : e + 1] = pos_ref[e, pl.ds(which, 1)]
            send_pos[side, s, 3:4] = species_ref[pl.ds(which, 1)].astype(F32)
    pl.semaphore_wait(barrier, 2)
    pos_dst = (recv_pos.at[0], recv_pos.at[1])
    pos_copies = exchange(0, send_pos.at[0], send_pos.at[1], pos_dst)

    centers = [tiles_ref[0, t] for t in range(cap)]
    partners = [tiles_ref[1, t] for t in range(cap)]
    none = jnp.int32(cap)
    for row, ids, how_many in ((0, centers, clusters), (1, partners, ext)):
        for t in range(cap):
            found = none
            for s in range(t):
                found = jnp.where(ids[s] == ids[t], jnp.int32(s), found)
            links[row, t] = found
        for g in range(how_many):
            found = none
            for s in range(cap):
                found = jnp.where(ids[s] == g, jnp.int32(s), found)
            links[2 + row, g] = found
    for side in range(2):
        for g in range(clusters):
            found = jnp.int32(margin)
            for s in range(margin):
                found = jnp.where(border_ref[side, s] == g, jnp.int32(s), found)
            links[4 + side, g] = found

    def spread_row(row):
        return jnp.broadcast_to(row, (size, size)).T

    for k in range(bases):
        scale_one[k] = message_scale * spread_row(radial_one_ref[k : k + 1])
        scale_two[k] = message_scale * spread_row(radial_two_ref[k : k + 1])
    total[cap] = jnp.zeros(total.shape[1:], F32)
    second[cap] = jnp.zeros(second.shape[1:], F32)
    for side in range(2):
        recv_grad[side, margin] = jnp.zeros(recv_grad.shape[2:], BF16)
        recv_move[side, margin] = jnp.zeros(recv_move.shape[2:], F32)
    moves[...] = jnp.zeros(moves.shape, F32)
    kinds = embed_ref.shape[0]
    kind_row = lax.broadcasted_iota(jnp.int32, (kinds, size), 0)

    def prepare(x):
        here = pos_ext[x]
        for e in range(3):
            spread_pos[x, e] = spread_row(here[e : e + 1])
        onehot = (kind_row == here[3:4].astype(jnp.int32)).astype(F32).astype(BF16)
        first = dot(embed_ref[...], onehot, TN)
        feat_t[x] = first
        feat[x] = first.T.astype(BF16)
        for k in range(bases):
            high, low = split(scale_one[k] * first)
            lift_one[x, 0:size, cols(k)] = high
            lift_one[x, size:, cols(k)] = low

    for i in range(clusters):
        for e in range(3):
            pos_ext[margin + i, e : e + 1] = pos_ref[e, i : i + 1]
        pos_ext[margin + i, 3:4] = species_ref[i : i + 1].astype(F32)
    pl.loop(margin, margin + clusters)(prepare)
    finish(pos_copies)
    for s in range(margin):
        pos_ext[s] = recv_pos[0, s]
        pos_ext[margin + clusters + s] = recv_pos[1, s]
    pl.loop(0, margin)(prepare)
    pl.loop(margin + clusters, ext)(prepare)

    eye = (
        lax.broadcasted_iota(jnp.int32, (size, size), 0)
        == lax.broadcasted_iota(jnp.int32, (size, size), 1)
    ).astype(F32)

    @pl.loop(0, cap)
    def _(t):
        center = tiles_ref[0, t]
        partner = tiles_ref[1, t]
        live = (t < count_ref[0]).astype(F32)
        same = live * (partner == center + margin).astype(F32)
        here = pos_ext[center + margin]
        u = [spread_pos[partner, e] - here[e : e + 1] for e in range(3)]
        square = u[0] * u[0] + u[1] * u[1] + u[2] * u[2] + soften
        inverse = lax.rsqrt(square)
        rho = square * inverse
        inside = jnp.maximum(1.0 - square * (1.0 / cutoff**2), 0.0)
        x = (rho - first_center) * (1.0 / spread)
        phi = jnp.exp(-x * x) * (inside * inside) * (live - same * eye)
        step = jnp.exp((2.0 * ratio) * x)
        y = [c * inverse for c in u]
        safe = jnp.where(inside > 0.0, inside, 1.0)
        slope = jnp.where(inside > 0.0, (-4.0 / cutoff**2) * rho / safe, 0.0)
        direction[t, 0] = y[0]
        direction[t, 1] = y[1]
        direction[t, 2] = y[2]
        direction[t, 3] = inverse
        direction[t, 4] = slope - (2.0 / spread) * x
        for k in range(bases):
            scaled = phi * math.exp(-((k * ratio) ** 2))
            radial[t, k] = scaled
            kern[t, 0, k] = scaled.astype(BF16)
            for m in range(3):
                kern[t, 1 + m, k] = (scaled * y[m]).astype(BF16)
            if k + 1 < bases:
                phi = phi * step

        before = links[0, t]
        for m in range(0, 4, 2):
            parts = None
            for k in range(0, bases, 2):
                block = jnp.concatenate(
                    [
                        jnp.concatenate([kern[t, m, k], kern[t, m + 1, k]], axis=1),
                        jnp.concatenate([kern[t, m, k + 1], kern[t, m + 1, k + 1]], axis=1),
                    ],
                    axis=0,
                )
                part = dot(lift_one[partner, :, cols(k, 2)], block)
                parts = part if parts is None else parts + part
            total[t, :, cols(m, 2)] = total[before, :, cols(m, 2)] + (parts[0:size] + parts[size:])

    mix_one_t = mix_one_ref[...].astype(F32).T.astype(BF16)
    mix_two_t = mix_two_ref[...].astype(F32).T.astype(BF16)

    @pl.loop(0, clusters)
    def _(g):
        last = links[2, g]
        mixed = dot(mix_one_t, total[last].astype(BF16))
        layer_t[margin + g, :, cols(0)] = (mixed[:, cols(0)] + feat_t[margin + g]).astype(BF16)
        layer_t[margin + g, :, cols(1, 3)] = mixed[:, cols(1, 3)].astype(BF16)

    for side in range(2):
        for s in range(margin):
            send_feat[side, s] = layer_t[margin + border_ref[side, s]]
    feat_dst = (recv_feat.at[0], recv_feat.at[1])
    feat_copies = exchange(1, send_feat.at[0], send_feat.at[1], feat_dst)

    def turn(x):
        for m in range(4):
            layer[x, m] = layer_t[x, :, cols(m)].astype(F32).T.astype(BF16)

    @pl.loop(0, clusters)
    def _(g):
        turn(margin + g)
        for m in range(4):
            desc_ref[g, m] = layer[margin + g, m]

    finish(feat_copies)
    for s in range(margin):
        layer_t[s] = recv_feat[0, s]
        layer_t[margin + clusters + s] = recv_feat[1, s]

    @pl.loop(0, cap)
    def _(t):
        partner = tiles_ref[1, t]
        message = second[links[0, t]]
        for k in range(0, bases, 2):
            parts = None
            for m in range(0, 4, 2):
                block = jnp.concatenate(
                    [
                        jnp.concatenate([kern[t, m, k], kern[t, m, k + 1]], axis=1),
                        jnp.concatenate([kern[t, m + 1, k], kern[t, m + 1, k + 1]], axis=1),
                    ],
                    axis=0,
                )
                part = dot(layer_t[partner, :, cols(m, 2)], block)
                parts = part if parts is None else parts + part
            message = message + scale_two[k] * parts[:, cols(0)] + scale_two[k + 1] * parts[:, cols(1)]
        second[t] = message

    readout_wide = spread_row(readout_ref[...].astype(F32))

    @pl.loop(0, clusters)
    def _(g):
        last = links[2, g]
        activation = dot(mix_two_t, second[last].astype(BF16))
        activation = activation + layer_t[margin + g, :, cols(0)].astype(F32)
        for m in range(1, 4):
            vector = layer_t[margin + g, :, cols(m)].astype(F32)
            activation = activation + vector * vector
        sigmoid = 1.0 / (1.0 + jnp.exp(-activation))
        energy_ref[pl.ds(g, 1)] = jnp.sum(
            activation * sigmoid * readout_wide, axis=0, keepdims=True
        )
        energy_t = readout_wide * sigmoid * (1.0 + activation * (1.0 - sigmoid))
        high, low = split(energy_t)
        adjoint_t = dot(mix_two_ref[...], high) + dot(mix_two_ref[...], low)
        adjoint = adjoint_t.T
        for k in range(bases):
            adj_two_t[g, :, cols(k)] = (scale_two[k] * adjoint_t).astype(BF16)
            adj_two[g, cols(k), :] = (
                (message_scale * radial_two_ref[k : k + 1]) * adjoint
            ).astype(BF16)
        energy_grad = energy_t.T
        direct[g, cols(0), :] = energy_grad
        for m in range(1, 4):
            direct[g, cols(m), :] = 2.0 * layer[margin + g, m].astype(F32) * energy_grad

    @pl.loop(0, cap)
    def _(t):
        center = tiles_ref[0, t]
        before = links[1, t]
        for m in range(4):
            parts = None
            for k in range(0, bases, 2):
                block = jnp.concatenate([kern[t, m, k], kern[t, m, k + 1]], axis=1)
                part = dot(block, adj_two[center, cols(k, 2), :])
                parts = part if parts is None else parts + part
            total[t, :, cols(m)] = total[before, :, cols(m)] + parts

    for side, start in enumerate((0, margin + clusters)):
        for s in range(margin):
            send_grad[side, s] = total[links[3, start + s]].astype(BF16)
    grad_dst = (recv_grad.at[0, pl.ds(0, margin)], recv_grad.at[1, pl.ds(0, margin)])
    grad_copies = exchange(2, send_grad.at[0], send_grad.at[1], grad_dst)
    pl.loop(0, margin)(turn)
    pl.loop(margin + clusters, ext)(turn)
    finish(grad_copies)

    @pl.loop(0, clusters)
    def _(g):
        last = links[3, margin + g]
        from_left = links[4, g]
        from_right = links[5, g]
        for m in range(4):
            grad = (
                direct[g, cols(m), :]
                + total[last, :, cols(m)]
                + recv_grad[0, from_left, :, cols(m)].astype(F32)
                + recv_grad[1, from_right, :, cols(m)].astype(F32)
            )
            high, low = split(grad)
            first_t = dot(mix_one_ref[...], high, NT) + dot(mix_one_ref[...], low, NT)
            for k in range(bases):
                adj_one_t[g, m, :, cols(k)] = (scale_one[k] * first_t).astype(BF16)

    rows8 = lax.broadcasted_iota(jnp.int32, moves.shape, 0)

    @pl.loop(0, cap)
    def _(t):
        center = tiles_ref[0, t]
        partner = tiles_ref[1, t]
        y = [direction[t, e] for e in range(3)]
        lhs = [jnp.concatenate([layer[partner, m], feat[partner]], axis=1) for m in range(4)]
        along = jnp.zeros((size, size), F32)
        ramp = jnp.zeros((size, size), F32)
        across = [jnp.zeros((size, size), F32) for _ in range(3)]
        for k in reversed(range(0, bases, 2)):
            grads = []
            for m in range(4):
                rhs = jnp.concatenate(
                    [adj_two_t[center, :, cols(k, 2)], adj_one_t[center, m, :, cols(k, 2)]], axis=0
                )
                grads.append(dot(lhs[m], rhs))
            for j in (1, 0):
                phi = radial[t, k + j]
                part = [grad[:, cols(j)] for grad in grads]
                mixed = part[0] + y[0] * part[1] + y[1] * part[2] + y[2] * part[3]
                along = along + phi * mixed
                if k + j:
                    ramp = ramp + along
                for e in range(3):
                    across[e] = across[e] + phi * part[1 + e]
        inverse = direction[t, 3]
        stretch = along * direction[t, 4] + (2.0 * ratio / spread) * ramp
        stretch = stretch - inverse * (y[0] * across[0] + y[1] * across[1] + y[2] * across[2])
        at_center = []
        at_partner = []
        for e in range(3):
            pull = stretch * y[e] + inverse * across[e]
            at_center.append(jnp.sum(pull, axis=0, keepdims=True))
            at_partner.append(jnp.sum(pull.T, axis=0, keepdims=True))
        pad = jnp.zeros((5, size), F32)
        gone = jnp.concatenate(at_center + [pad], axis=0)
        came = jnp.concatenate(at_partner + [pad], axis=0)
        moves[...] = (
            moves[...]
            - jnp.where(rows8 == center + margin, gone[None], 0.0)
            + jnp.where(rows8 == partner, came[None], 0.0)
        )

    move_dst = (recv_move.at[0, pl.ds(0, margin)], recv_move.at[1, pl.ds(0, margin)])
    move_copies = exchange(
        3, moves.at[pl.ds(0, margin)], moves.at[pl.ds(margin + clusters, margin)], move_dst
    )
    finish(move_copies)
    for g in range(clusters):
        moved = moves[margin + g] + recv_move[0, links[4, g]] + recv_move[1, links[5, g]]
        for e in range(3):
            forces_ref[e, g : g + 1] = -moved[e : e + 1]


def shards(
    n,
    positions,
    species,
    element_embed,
    radial_one,
    mix_one,
    radial_two,
    mix_two,
    readout,
    tile_list,
    tile_count,
    border,
):
    clusters, _, size = positions.shape
    channels = element_embed.shape[1]
    bases = radial_one.shape[0]
    margin = border.shape[1]
    cap = tile_list.shape[0]
    ext = clusters + 2 * margin
    smem = pl.BlockSpec(memory_space=pltpu.SMEM)
    vmem = pl.BlockSpec(memory_space=pltpu.VMEM)
    hbm = pl.BlockSpec(memory_space=pltpu.HBM)
    arrays = (
        jnp.transpose(positions, (1, 0, 2)),
        species,
        element_embed,
        radial_one,
        mix_one,
        radial_two,
        mix_two,
        readout.reshape(1, channels),
    )
    square = (size, size)
    wide = 4 * size
    energy, forces, descriptors = pl.pallas_call(
        functools.partial(body, (n, clusters, margin, cap, bases, size)),
        out_shape=(
            jax.ShapeDtypeStruct((clusters, size), F32),
            jax.ShapeDtypeStruct((3, clusters, size), F32),
            jax.ShapeDtypeStruct((clusters, 4, size, channels), BF16),
        ),
        in_specs=[smem] * 3 + [hbm] * len(arrays),
        out_specs=(vmem, vmem, vmem),
        scratch_shapes=[
            pltpu.SMEM((6, 16), jnp.int32),
            *[pltpu.VMEM(array.shape, array.dtype) for array in arrays],
            pltpu.SemaphoreType.DMA((len(arrays),)),
            pltpu.VMEM((2, margin, 4, size), F32),
            pltpu.VMEM((2, margin, 4, size), F32),
            pltpu.VMEM((2, margin, channels, wide), BF16),
            pltpu.VMEM((2, margin, channels, wide), BF16),
            pltpu.VMEM((2, margin, size, wide), BF16),
            pltpu.VMEM((2, margin + 1, size, wide), BF16),
            pltpu.VMEM((2, margin + 1, 8, size), F32),
            pltpu.VMEM((ext, 4, size), F32),
            pltpu.VMEM((ext, 3) + square, F32),
            pltpu.VMEM((bases,) + square, F32),
            pltpu.VMEM((bases,) + square, F32),
            pltpu.VMEM((ext,) + square, F32),
            pltpu.VMEM((ext,) + square, BF16),
            pltpu.VMEM((ext, 2 * channels, bases * size), BF16),
            pltpu.VMEM((ext, channels, wide), BF16),
            pltpu.VMEM((ext, 4) + square, BF16),
            pltpu.VMEM((cap, 4, bases) + square, BF16),
            pltpu.VMEM((cap, bases) + square, F32),
            pltpu.VMEM((cap, 5) + square, F32),
            pltpu.VMEM((cap + 1, channels, wide), F32),
            pltpu.VMEM((cap + 1,) + square, F32),
            pltpu.VMEM((clusters, bases * size, channels), BF16),
            pltpu.VMEM((clusters, channels, bases * size), BF16),
            pltpu.VMEM((clusters, 4, channels, bases * size), BF16),
            pltpu.VMEM((clusters, wide, channels), F32),
            pltpu.VMEM((ext, 8, size), F32),
            pltpu.SemaphoreType.DMA((4, 2)),
            pltpu.SemaphoreType.DMA((4, 2)),
        ],
        compiler_params=pltpu.CompilerParams(
            collective_id=0, has_side_effects=True, vmem_limit_bytes=61 * 1024 * 1024
        ),
    )(
        tile_list.T,
        tile_count,
        border,
        *arrays,
    )
    return energy, jnp.transpose(forces, (1, 0, 2)), descriptors


def solution(mesh):
    placed = (
        P(("rep", "bx"), None, None),
        P(("rep", "bx"), None),
        P(),
        P(),
        P(),
        P(),
        P(),
        P(),
        P(("rep", "bx"), None),
        P(("rep", "bx")),
        P(("rep", "bx"), None),
    )
    return jax.shard_map(
        functools.partial(shards, mesh.shape["bx"]),
        mesh=mesh,
        in_specs=placed,
        out_specs=(
            P(("rep", "bx"), None),
            P(("rep", "bx"), None, None),
            P(("rep", "bx"), None, None, None),
        ),
        check_vma=False,
    )
```

profile of v0, /device:TPU:46, one launch (start us, length us, event | category | flops | bytes accessed | tf_op | source)
XLA Modules:
  0.0 76.1 jit_solution(5676548809544254861)
XLA Ops:
  1.3 71.1 %shard_map.130 = (f32[4,128]{1,0:T(4,128)}, f32[3,4,128]{2,1,0:T(4,128)}, bf16[4,4,128,128]{3,2,1,0:T(8,128)(2,1)}) custom-call(s32[2,12]{1,0:T(2,128)} %bitcast.6, s32[1]{0:T(128)S(6)} %copy.17.count_ref, s32[2,2]{1,0:T(2,128)} %border_ref.1, f32[3,4,128]{2,1,0:T(4,128)} %bitcast.5, s32[4,128]{1,0:T(4,128)} %species_far.1, bf16[89,128]{1,0:T(8,128)(2,1)} %embed_far.1, ...), custom_call_target="tpu_custom_call" | custom-call | tf_op jit(solution)/shard_map/pallas_call | solution.py:469
  72.4 0.0 copy-start
  72.4 1.2 %copy.18 = f32[4,128]{1,0:T(4,128)} copy(f32[4,128]{1,0:T(4,128)} %get-tuple-element.12) | data formatting | bytes 4096
  73.6 0.0 copy-done
  73.6 0.6 copy.19
  74.2 1.9 %copy.20 = bf16[4,4,128,128]{3,2,1,0:T(8,128)(2,1)} copy(bf16[4,4,128,128]{3,2,1,0:T(8,128)(2,1)} %get-tuple-element.14) | data formatting | bytes 1048576
Async XLA Ops:
  72.4 1.3 %copy-start = (f32[3,4,128]{2,1,0:T(4,128)S(1)}, f32[3,4,128]{2,1,0:T(4,128)}, u32[]{:S(2)}) copy-start(f32[3,4,128]{2,1,0:T(4,128)} %get-tuple-element.7) | copy-start | bytes 18436
where the time goes:
time: 76.4 us; the launch traced here: 76.1 us
  Pallas kernels  71.1 us (93%)
  local copies, waits for them, and re-layouts  3.73 us (5%)
  between operations  1.3 us (2%)
    pallas_call x1, Pallas kernels, shards(): pl.pallas_call(functools.partial(body, (n, clusters, margin, cap, bases,...  71.1 us
    unnamed x5, local copies, waits for them, and re-layouts  3.73 us

commit v1 on v0

--- a/solution.py
+++ b/solution.py
@@ -19,6 +19,9 @@
 center_step = 0.45
 message_scale = 0.125
 ratio = center_step / spread
+
+GROUP = 4
+ROWS = 16
 
 NN = (((1,), (0,)), ((), ()))
 NT = (((1,), (1,)), ((), ()))
@@ -60,6 +63,7 @@
     mix_two_ref,
     readout_ref,
     load_sem,
+    store_sem,
     send_pos,
     recv_pos,
     send_feat,
@@ -76,7 +80,9 @@
     lift_one,
     layer_t,
     layer,
-    kern,
+    diagonal,
+    grads_even,
+    grads_odd,
     radial,
     direction,
     total,
@@ -88,8 +94,11 @@
     moves,
     send_sem,
     recv_sem,
+    *kerns,
 ):
     n, clusters, margin, cap, bases, size = sizes
+    group = len(kerns)
+    rounds = cap // group
     ext = clusters + 2 * margin
     me = lax.axis_index("bx")
     rep = lax.axis_index("rep")
@@ -99,20 +108,17 @@
     def cols(i, width=1):
         return slice(i * size, (i + width) * size)
 
-    def exchange(step, src_left, src_right, dst):
-        out = []
-        for side, (src, target) in enumerate(((src_left, left), (src_right, right))):
-            copy = pltpu.make_async_remote_copy(
-                src_ref=src,
-                dst_ref=dst[1 - side],
-                send_sem=send_sem.at[step, side],
-                recv_sem=recv_sem.at[step, 1 - side],
-                device_id=(rep, target),
-                device_id_type=MESH,
-            )
-            copy.start()
-            out.append(copy)
-        return out
+    def push(step, side, src, dst, piece=0):
+        copy = pltpu.make_async_remote_copy(
+            src_ref=src,
+            dst_ref=dst,
+            send_sem=send_sem.at[step, side, piece],
+            recv_sem=recv_sem.at[step, 1 - side, piece],
+            device_id=(rep, (left, right)[side]),
+            device_id_type=MESH,
+        )
+        copy.start()
+        return copy
 
     def finish(copies):
         for copy in copies:
@@ -143,8 +149,7 @@
                 send_pos[side, s, e : e + 1] = pos_ref[e, pl.ds(which, 1)]
             send_pos[side, s, 3:4] = species_ref[pl.ds(which, 1)].astype(F32)
     pl.semaphore_wait(barrier, 2)
-    pos_dst = (recv_pos.at[0], recv_pos.at[1])
-    pos_copies = exchange(0, send_pos.at[0], send_pos.at[1], pos_dst)
+    pos_copies = [push(0, side, send_pos.at[side], recv_pos.at[1 - side]) for side in range(2)]
 
     centers = [tiles_ref[0, t] for t in range(cap)]
     partners = [tiles_ref[1, t] for t in range(cap)]
@@ -207,73 +212,90 @@
     pl.loop(0, margin)(prepare)
     pl.loop(margin + clusters, ext)(prepare)
 
-    eye = (
+    diagonal[...] = (
         lax.broadcasted_iota(jnp.int32, (size, size), 0)
         == lax.broadcasted_iota(jnp.int32, (size, size), 1)
     ).astype(F32)
 
-    @pl.loop(0, cap)
-    def _(t):
+    def pair(t):
         center = tiles_ref[0, t]
         partner = tiles_ref[1, t]
-        live = (t < count_ref[0]).astype(F32)
+        live = (t < count_ref[0, 0]).astype(F32)
         same = live * (partner == center + margin).astype(F32)
+        return center, partner, live, same
+
+    def geometry(center, partner, live, same, rows):
         here = pos_ext[center + margin]
-        u = [spread_pos[partner, e] - here[e : e + 1] for e in range(3)]
+        u = [spread_pos[partner, e, rows] - here[e : e + 1] for e in range(3)]
         square = u[0] * u[0] + u[1] * u[1] + u[2] * u[2] + soften
         inverse = lax.rsqrt(square)
         rho = square * inverse
         inside = jnp.maximum(1.0 - square * (1.0 / cutoff**2), 0.0)
         x = (rho - first_center) * (1.0 / spread)
-        phi = jnp.exp(-x * x) * (inside * inside) * (live - same * eye)
+        phi = jnp.exp(-x * x) * (inside * inside) * (live - same * diagonal[rows])
         step = jnp.exp((2.0 * ratio) * x)
-        y = [c * inverse for c in u]
-        safe = jnp.where(inside > 0.0, inside, 1.0)
-        slope = jnp.where(inside > 0.0, (-4.0 / cutoff**2) * rho / safe, 0.0)
-        direction[t, 0] = y[0]
-        direction[t, 1] = y[1]
-        direction[t, 2] = y[2]
-        direction[t, 3] = inverse
-        direction[t, 4] = slope - (2.0 / spread) * x
+        scaled = []
         for k in range(bases):
-            scaled = phi * math.exp(-((k * ratio) ** 2))
-            radial[t, k] = scaled
-            kern[t, 0, k] = scaled.astype(BF16)
-            for m in range(3):
-                kern[t, 1 + m, k] = (scaled * y[m]).astype(BF16)
-            if k + 1 < bases:
-                phi = phi * step
-
-        before = links[0, t]
-        for m in range(0, 4, 2):
-            parts = None
-            for k in range(0, bases, 2):
-                block = jnp.concatenate(
-                    [
-                        jnp.concatenate([kern[t, m, k], kern[t, m + 1, k]], axis=1),
-                        jnp.concatenate([kern[t, m, k + 1], kern[t, m + 1, k + 1]], axis=1),
-                    ],
-                    axis=0,
-                )
-                part = dot(lift_one[partner, :, cols(k, 2)], block)
-                parts = part if parts is None else parts + part
-            total[t, :, cols(m, 2)] = total[before, :, cols(m, 2)] + (parts[0:size] + parts[size:])
+            scaled.append(phi * math.exp(-((k * ratio) ** 2)))
+            phi = phi * step
+        return scaled, [c * inverse for c in u], inverse, rho, inside, x
+
+    blocks = [slice(r, r + ROWS) for r in range(0, size, ROWS)]
+
+    @pl.loop(0, rounds)
+    def _(i):
+        def form(j):
+            what = pair(i * group + j)
+            for rows in blocks:
+                scaled, y = geometry(*what, rows)[:2]
+                for k in range(bases):
+                    kerns[j][i, 0, k, rows] = scaled[k].astype(BF16)
+                    for m in range(3):
+                        kerns[j][i, 1 + m, k, rows] = (scaled[k] * y[m]).astype(BF16)
+
+        def gather(j):
+            t = i * group + j
+            kern = kerns[j]
+            partner = tiles_ref[1, t]
+            before = links[0, t]
+            for m in range(0, 4, 2):
+                parts = None
+                for k in range(0, bases, 2):
+                    block = jnp.concatenate(
+                        [
+                            jnp.concatenate([kern[i, m, k], kern[i, m + 1, k]], axis=1),
+                            jnp.concatenate([kern[i, m, k + 1], kern[i, m + 1, k + 1]], axis=1),
+                        ],
+                        axis=0,
+                    )
+                    part = dot(lift_one[partner, :, cols(k, 2)], block)
+                    parts = part if parts is None else parts + part
+                total[t, :, cols(m, 2)] = total[before, :, cols(m, 2)] + (parts[0:size] + parts[size:])
+
+        form(0)
+        for j in range(group):
+            if j + 1 < group:
+                form(j + 1)
+            gather(j)
 
     mix_one_t = mix_one_ref[...].astype(F32).T.astype(BF16)
     mix_two_t = mix_two_ref[...].astype(F32).T.astype(BF16)
 
+    def layer_of(g, out):
+        mixed = dot(mix_one_t, total[links[2, g]].astype(BF16))
+        out[:, cols(0)] = (mixed[:, cols(0)] + feat_t[margin + g]).astype(BF16)
+        out[:, cols(1, 3)] = mixed[:, cols(1, 3)].astype(BF16)
+
+    feat_copies = []
+    for s in range(margin):
+        for side in range(2):
+            layer_of(border_ref[side, s], send_feat.at[side, s])
+        for side in range(2):
+            feat_copies.append(push(1, side, send_feat.at[side, s], recv_feat.at[1 - side, s], s))
+
     @pl.loop(0, clusters)
     def _(g):
-        last = links[2, g]
-        mixed = dot(mix_one_t, total[last].astype(BF16))
-        layer_t[margin + g, :, cols(0)] = (mixed[:, cols(0)] + feat_t[margin + g]).astype(BF16)
-        layer_t[margin + g, :, cols(1, 3)] = mixed[:, cols(1, 3)].astype(BF16)
-
-    for side in range(2):
-        for s in range(margin):
-            send_feat[side, s] = layer_t[margin + border_ref[side, s]]
-    feat_dst = (recv_feat.at[0], recv_feat.at[1])
-    feat_copies = exchange(1, send_feat.at[0], send_feat.at[1], feat_dst)
+        layer_of(g, layer_t.at[margin + g])
 
     def turn(x):
         for m in range(4):
@@ -282,32 +304,51 @@
     @pl.loop(0, clusters)
     def _(g):
         turn(margin + g)
-        for m in range(4):
-            desc_ref[g, m] = layer[margin + g, m]
+
+    store = pltpu.make_async_copy(layer.at[pl.ds(margin, clusters)], desc_ref, store_sem)
+    store.start()
+
+    @pl.loop(0, cap)
+    def _(t):
+        what = pair(t)
+        for rows in blocks:
+            scaled, y, inverse, rho, inside, x = geometry(*what, rows)
+            safe = jnp.where(inside > 0.0, inside, 1.0)
+            slope = jnp.where(inside > 0.0, (-4.0 / cutoff**2) * rho / safe, 0.0)
+            for k in range(bases):
+                radial[t, k, rows] = scaled[k]
+            for e in range(3):
+                direction[t, e, rows] = y[e]
+            direction[t, 3, rows] = inverse
+            direction[t, 4, rows] = slope - (2.0 / spread) * x
 
     finish(feat_copies)
     for s in range(margin):
         layer_t[s] = recv_feat[0, s]
         layer_t[margin + clusters + s] = recv_feat[1, s]
 
-    @pl.loop(0, cap)
-    def _(t):
-        partner = tiles_ref[1, t]
-        message = second[links[0, t]]
-        for k in range(0, bases, 2):
-            parts = None
-            for m in range(0, 4, 2):
-                block = jnp.concatenate(
-                    [
-                        jnp.concatenate([kern[t, m, k], kern[t, m, k + 1]], axis=1),
-                        jnp.concatenate([kern[t, m + 1, k], kern[t, m + 1, k + 1]], axis=1),
-                    ],
-                    axis=0,
-                )
-                part = dot(layer_t[partner, :, cols(m, 2)], block)
-                parts = part if parts is None else parts + part
-            message = message + scale_two[k] * parts[:, cols(0)] + scale_two[k + 1] * parts[:, cols(1)]
-        second[t] = message
+    @pl.loop(0, rounds)
+    def _(i):
+        for j in range(group):
+            t = i * group + j
+            kern = kerns[j]
+            partner = tiles_ref[1, t]
+            message = None
+            for k in range(0, bases, 2):
+                parts = None
+                for m in range(0, 4, 2):
+                    block = jnp.concatenate(
+                        [
+                            jnp.concatenate([kern[i, m, k], kern[i, m, k + 1]], axis=1),
+                            jnp.concatenate([kern[i, m + 1, k], kern[i, m + 1, k + 1]], axis=1),
+                        ],
+                        axis=0,
+                    )
+                    part = dot(layer_t[partner, :, cols(m, 2)], block)
+                    parts = part if parts is None else parts + part
+                more = scale_two[k] * parts[:, cols(0)] + scale_two[k + 1] * parts[:, cols(1)]
+                message = more if message is None else message + more
+            second[t] = second[links[0, t]] + message
 
     readout_wide = spread_row(readout_ref[...].astype(F32))
 
@@ -337,23 +378,27 @@
         for m in range(1, 4):
             direct[g, cols(m), :] = 2.0 * layer[margin + g, m].astype(F32) * energy_grad
 
-    @pl.loop(0, cap)
-    def _(t):
-        center = tiles_ref[0, t]
-        before = links[1, t]
-        for m in range(4):
-            parts = None
-            for k in range(0, bases, 2):
-                block = jnp.concatenate([kern[t, m, k], kern[t, m, k + 1]], axis=1)
-                part = dot(block, adj_two[center, cols(k, 2), :])
-                parts = part if parts is None else parts + part
-            total[t, :, cols(m)] = total[before, :, cols(m)] + parts
+    @pl.loop(0, rounds)
+    def _(i):
+        for j in range(group):
+            t = i * group + j
+            kern = kerns[j]
+            center = tiles_ref[0, t]
+            before = links[1, t]
+            for m in range(4):
+                parts = None
+                for k in range(0, bases, 2):
+                    block = jnp.concatenate([kern[i, m, k], kern[i, m, k + 1]], axis=1)
+                    part = dot(block, adj_two[center, cols(k, 2), :])
+                    parts = part if parts is None else parts + part
+                total[t, :, cols(m)] = total[before, :, cols(m)] + parts
 
     for side, start in enumerate((0, margin + clusters)):
         for s in range(margin):
             send_grad[side, s] = total[links[3, start + s]].astype(BF16)
-    grad_dst = (recv_grad.at[0, pl.ds(0, margin)], recv_grad.at[1, pl.ds(0, margin)])
-    grad_copies = exchange(2, send_grad.at[0], send_grad.at[1], grad_dst)
+    grad_copies = [
+        push(2, side, send_grad.at[side], recv_grad.at[1 - side, pl.ds(0, margin)]) for side in range(2)
+    ]
     pl.loop(0, margin)(turn)
     pl.loop(margin + clusters, ext)(turn)
     finish(grad_copies)
@@ -377,58 +422,82 @@
 
     rows8 = lax.broadcasted_iota(jnp.int32, moves.shape, 0)
 
-    @pl.loop(0, cap)
-    def _(t):
+    def grads_of(t, out):
         center = tiles_ref[0, t]
         partner = tiles_ref[1, t]
-        y = [direction[t, e] for e in range(3)]
-        lhs = [jnp.concatenate([layer[partner, m], feat[partner]], axis=1) for m in range(4)]
-        along = jnp.zeros((size, size), F32)
-        ramp = jnp.zeros((size, size), F32)
-        across = [jnp.zeros((size, size), F32) for _ in range(3)]
-        for k in reversed(range(0, bases, 2)):
-            grads = []
-            for m in range(4):
+        for m in range(4):
+            lhs = jnp.concatenate([layer[partner, m], feat[partner]], axis=1)
+            for k in range(0, bases, 2):
                 rhs = jnp.concatenate(
                     [adj_two_t[center, :, cols(k, 2)], adj_one_t[center, m, :, cols(k, 2)]], axis=0
                 )
-                grads.append(dot(lhs[m], rhs))
-            for j in (1, 0):
-                phi = radial[t, k + j]
-                part = [grad[:, cols(j)] for grad in grads]
-                mixed = part[0] + y[0] * part[1] + y[1] * part[2] + y[2] * part[3]
-                along = along + phi * mixed
-                if k + j:
-                    ramp = ramp + along
+                out[m, :, cols(k, 2)] = dot(lhs, rhs)
+
+    def force(t, grads):
+        center = tiles_ref[0, t]
+        partner = tiles_ref[1, t]
+        at_center = [None] * 3
+        whole = [[], [], []]
+        for rows in blocks:
+            y = [direction[t, e, rows] for e in range(3)]
+            along = ramp = None
+            across = [None] * 3
+            for k in reversed(range(bases)):
+                phi = radial[t, k, rows]
+                part = [grads[m, rows, cols(k)] for m in range(4)]
+                mixed = phi * (part[0] + y[0] * part[1] + y[1] * part[2] + y[2] * part[3])
+                along = mixed if along is None else along + mixed
+                if k:
+                    ramp = along if ramp is None else ramp + along
                 for e in range(3):
-                    across[e] = across[e] + phi * part[1 + e]
-        inverse = direction[t, 3]
-        stretch = along * direction[t, 4] + (2.0 * ratio / spread) * ramp
-        stretch = stretch - inverse * (y[0] * across[0] + y[1] * across[1] + y[2] * across[2])
-        at_center = []
-        at_partner = []
-        for e in range(3):
-            pull = stretch * y[e] + inverse * across[e]
-            at_center.append(jnp.sum(pull, axis=0, keepdims=True))
-            at_partner.append(jnp.sum(pull.T, axis=0, keepdims=True))
+                    pull = phi * part[1 + e]
+                    across[e] = pull if across[e] is None else across[e] + pull
+            inverse = direction[t, 3, rows]
+            stretch = along * direction[t, 4, rows] + (2.0 * ratio / spread) * ramp
+            stretch = stretch - inverse * (y[0] * across[0] + y[1] * across[1] + y[2] * across[2])
+            for e in range(3):
+                pull = stretch * y[e] + inverse * across[e]
+                whole[e].append(pull)
+                at_center[e] = pull if at_center[e] is None else at_center[e] + pull
+        at_center = [jnp.sum(pull, axis=0, keepdims=True) for pull in at_center]
+        at_partner = [
+            jnp.sum(jnp.concatenate(pulls, axis=0).T, axis=0, keepdims=True) for pulls in whole
+        ]
         pad = jnp.zeros((5, size), F32)
         gone = jnp.concatenate(at_center + [pad], axis=0)
         came = jnp.concatenate(at_partner + [pad], axis=0)
         moves[...] = (
             moves[...]
+            + jnp.where(rows8 == partner, came[None], 0.0)
             - jnp.where(rows8 == center + margin, gone[None], 0.0)
-            + jnp.where(rows8 == partner, came[None], 0.0)
         )
 
-    move_dst = (recv_move.at[0, pl.ds(0, margin)], recv_move.at[1, pl.ds(0, margin)])
-    move_copies = exchange(
-        3, moves.at[pl.ds(0, margin)], moves.at[pl.ds(margin + clusters, margin)], move_dst
-    )
+    grads_of(0, grads_even)
+
+    @pl.loop(0, cap // 2)
+    def _(i):
+        t = 2 * i
+        grads_of(t + 1, grads_odd)
+        force(t, grads_even)
+        grads_of(jnp.minimum(t + 2, cap - 1), grads_even)
+        force(t + 1, grads_odd)
+
+    starts = (0, margin + clusters)
+    move_copies = [
+        push(3, side, moves.at[pl.ds(starts[side], margin)], recv_move.at[1 - side, pl.ds(0, margin)])
+        for side in range(2)
+    ]
+    store.wait()
     finish(move_copies)
     for g in range(clusters):
         moved = moves[margin + g] + recv_move[0, links[4, g]] + recv_move[1, links[5, g]]
         for e in range(3):
             forces_ref[e, g : g + 1] = -moved[e : e + 1]
+
+
+def hand_over(*refs):
+    for src, dst in zip(refs[:3], refs[3:], strict=True):
+        dst[...] = src[...]
 
 
 def shards(
@@ -466,6 +535,7 @@
     )
     square = (size, size)
     wide = 4 * size
+    group = math.gcd(cap, GROUP)
     energy, forces, descriptors = pl.pallas_call(
         functools.partial(body, (n, clusters, margin, cap, bases, size)),
         out_shape=(
@@ -474,11 +544,12 @@
             jax.ShapeDtypeStruct((clusters, 4, size, channels), BF16),
         ),
         in_specs=[smem] * 3 + [hbm] * len(arrays),
-        out_specs=(vmem, vmem, vmem),
+        out_specs=(vmem, vmem, hbm),
         scratch_shapes=[
             pltpu.SMEM((6, 16), jnp.int32),
             *[pltpu.VMEM(array.shape, array.dtype) for array in arrays],
             pltpu.SemaphoreType.DMA((len(arrays),)),
+            pltpu.SemaphoreType.DMA,
             pltpu.VMEM((2, margin, 4, size), F32),
             pltpu.VMEM((2, margin, 4, size), F32),
             pltpu.VMEM((2, margin, channels, wide), BF16),
@@ -495,7 +566,9 @@
             pltpu.VMEM((ext, 2 * channels, bases * size), BF16),
             pltpu.VMEM((ext, channels, wide), BF16),
             pltpu.VMEM((ext, 4) + square, BF16),
-            pltpu.VMEM((cap, 4, bases) + square, BF16),
+            pltpu.VMEM(square, F32),
+            pltpu.VMEM((4, size, bases * size), F32),
+            pltpu.VMEM((4, size, bases * size), F32),
             pltpu.VMEM((cap, bases) + square, F32),
             pltpu.VMEM((cap, 5) + square, F32),
             pltpu.VMEM((cap + 1, channels, wide), F32),
@@ -505,18 +578,26 @@
             pltpu.VMEM((clusters, 4, channels, bases * size), BF16),
             pltpu.VMEM((clusters, wide, channels), F32),
             pltpu.VMEM((ext, 8, size), F32),
-            pltpu.SemaphoreType.DMA((4, 2)),
-            pltpu.SemaphoreType.DMA((4, 2)),
+            pltpu.SemaphoreType.DMA((4, 2, margin)),
+            pltpu.SemaphoreType.DMA((4, 2, margin)),
+            *[pltpu.VMEM((cap // group, 4, bases) + square, BF16) for _ in range(group)],
         ],
         compiler_params=pltpu.CompilerParams(
             collective_id=0, has_side_effects=True, vmem_limit_bytes=61 * 1024 * 1024
         ),
     )(
         tile_list.T,
-        tile_count,
+        tile_count.reshape(1, 1),
         border,
         *arrays,
     )
+    results = (energy, forces, descriptors)
+    energy, forces, descriptors = pl.pallas_call(
+        hand_over,
+        out_shape=tuple(jax.ShapeDtypeStruct(x.shape, x.dtype) for x in results),
+        in_specs=[vmem] * 3,
+        out_specs=(vmem, vmem, vmem),
+    )(*results)
     return energy, jnp.transpose(forces, (1, 0, 2)), descriptors
 
 

time: 76.4 us -> 68.8 us (0.901)
  Pallas kernels: 71.1 us -> 67.3 us
  local copies, waits for them, and re-layouts: 3.73 us -> 0 us
    pallas_call x1, Pallas kernels: 71.1 us -> 65.4 us  [shards(): pl.pallas_call(functools.partial(body, (n, clusters, margin, cap, bases,...]
    unnamed x5 -> x0, local copies, waits for them, and re-layouts: 3.73 us -> none
    pallas_call x0 -> x1, Pallas kernels: none -> 1.89 us  [shards(): pl.pallas_call(hand_over, out_shape=tuple((jax.ShapeDtypeStruct(x.shape,...]
where the time goes in v1:
time: 68.8 us; the launch traced here: 68.6 us
  Pallas kernels  67.3 us (98%)
  between operations  1.29 us (2%)
    pallas_call x1, Pallas kernels, shards(): pl.pallas_call(functools.partial(body, (n, clusters, margin, cap, bases,...  65.4 us
    pallas_call x1, Pallas kernels, shards(): pl.pallas_call(hand_over, out_shape=tuple((jax.ShapeDtypeStruct(x.shape,...  1.89 us

profile of v1, /device:TPU:46, one launch (start us, length us, event | category | flops | bytes accessed | tf_op | source)
XLA Modules:
  0.0 68.6 jit_solution(1425900922266784003)
XLA Ops:
  1.3 65.4 %shard_map.130 = (f32[4,128]{1,0:T(4,128)}, f32[3,4,128]{2,1,0:T(4,128)}, bf16[4,4,128,128]{3,2,1,0:T(8,128)(2,1)}) custom-call(s32[2,12]{1,0:T(2,128)} %bitcast.7, s32[1,1]{1,0:T(1,128)} %bitcast.5.count_ref, s32[2,2]{1,0:T(2,128)} %border_ref.1, f32[3,4,128]{2,1,0:T(4,128)} %bitcast.6, s32[4,128]{1,0:T(4,128)} %species_far.1, bf16[89,128]{1,0:T(8,128)(2,1)} %embed_far.1, ...), custom_call_target="tpu_custom_call" | custom-call | tf_op jit(solution)/shard_map/pallas_call | solution.py:539
  66.7 1.9 %shard_map.131 = (f32[4,128]{1,0:T(4,128)}, f32[3,4,128]{2,1,0:T(4,128)}, bf16[4,4,128,128]{3,2,1,0:T(8,128)(2,1)}) custom-call(f32[4,128]{1,0:T(4,128)} %get-tuple-element.9.refs_0_, f32[3,4,128]{2,1,0:T(4,128)} %get-tuple-element.10.refs_1_, bf16[4,4,128,128]{3,2,1,0:T(8,128)(2,1)} %get-tuple-element.11.refs_2_), custom_call_target="tpu_custom_call" | custom-call | tf_op jit(solution)/shard_map/pallas_call | solution.py:595
